TPU v7x, 32 devices: a whole 2x2x4 slice. The times are simulated.
32 devices in a mesh: dp: 2 (over x), expert: 4 (over z), seq: 4 (over y, core).
Axes of the slice: x: 2, y: 2, z: 4, core: 2. Of those that a mesh axis runs over, the one named last changes fastest.
Arguments:
- tokens: bfloat16 [4096, 1024], P(('dp', 'expert', 'seq')), parts along dimension 0, may hold values from -6 to 6
- picks: int32 [32, 4, 16], P(('dp', 'expert', 'seq')), parts along dimension 0, may hold values from 0 to 127, as said below
- gates: float32 [32, 4, 16], P(('dp', 'expert', 'seq')), parts along dimension 0, may hold values from 0.1 to 2
- counts: int32 [32, 4], P(('dp', 'expert', 'seq')), parts along dimension 0, may hold values from 1 to 16, as said below
- norm_in: float32 [1024], replicated, may hold values from 0.1 to 1.9
- norm_out: float32 [1024], replicated, may hold values from 0.1 to 1.9
- w_in: bfloat16 [4, 1024, 1408], P('expert'), may hold values from -0.1875 to 0.1875
- w_out: bfloat16 [4, 1408, 1024], P('expert'), may hold values from -0.15625 to 0.15625
- w_key: bfloat16 [1024, 512], replicated, may hold values from -0.1875 to 0.1875
- w_value: bfloat16 [1024, 512], replicated, may hold values from -0.1875 to 0.1875
- queries: bfloat16 [1024, 512], P(('dp', 'expert', 'seq')), parts along dimension 0, may hold values from -300 to 300
- w_proj: bfloat16 [512, 1024], replicated, may hold values from -0.25 to 0.25
Outputs:
- encoded: bfloat16 [4096, 1024], P(('dp', 'expert', 'seq')), parts along dimension 0
- dec_out: bfloat16 [1024, 1024], P(('dp', 'expert', 'seq')), parts along dimension 0
There are 2 independent parts, one for each index of `dp`. A program takes and returns all parts, laid end to end along the dimension named above; an argument that names none is the same for every part. Nothing has to cross between parts.
Inputs may be any that keep to these rules, and one draw needn't show every extreme that they name: `picks`: for each source device and expert, 16 different row numbers of that device's 128 tokens. Slots c < counts are live, the rest are padding; some source device and expert has all 16 slots live.
All inputs are finite; a program needn't handle non-finite values.
Results may differ from a plain program's by a relative error of at most 0.015.
The roundings to bfloat16 on the way count: a program that leaves them out, or rounds other values in their place, can miss the bound.
Values may be sent and summed in bfloat16 or wider, within the bound.
A program may use at most 64 MiB of HBM per device.

v0:
```python
import functools

import jax
import jax.numpy as jnp
from jax import lax
from jax.experimental import pallas as pl
from jax.experimental.pallas import tpu as pltpu
from jax.sharding import PartitionSpec as P

HEADS = 8
EPSILON = 1e-06
VMEM_BYTES = 67043328
MESH = pl.DeviceIdType.MESH
GATHER_PIECES = 1
RETURN_PIECES = 1
F32 = jnp.float32
BF16 = jnp.bfloat16


def rms_norm(values, gain):
    mean_square = jnp.mean(values * values, axis=-1, keepdims=True)
    return values * lax.rsqrt(mean_square + EPSILON) * gain


def gelu(v):
    return 0.5 * v * (1.0 + jnp.tanh(0.7978845608028654 * (v + 0.044715 * v * v * v)))


def kernel(
    n_e,
    n_s,
    tokens_h,
    picks_h,
    gates_h,
    counts_h,
    norm_in_h,
    norm_out_h,
    w_in_h,
    w_out_h,
    w_key_h,
    w_value_h,
    queries_h,
    w_proj_h,
    enc_v,
    part_r,
    w_proj_v,
    tokens_v,
    picks_v,
    gates_v,
    counts_v,
    norm_in_v,
    norm_out_v,
    w_in_v,
    w_out_v,
    w_key_v,
    w_value_v,
    q_v,
    send_a,
    recv_a,
    send_b,
    recv_b,
    part_v,
    load_sem,
    a_send,
    a_recv,
    b_send,
    b_recv,
    q_send,
    q_recv,
    p_send,
    p_recv,
):
    me_e = lax.axis_index("expert")
    me_s = lax.axis_index("seq")
    upper = (2 * me_e) // n_e
    rows, width = tokens_v.shape
    slots = send_a.shape[1]
    dec_rows = q_v.shape[1]
    q_width = q_v.shape[2]
    head = q_width // HEADS

    barrier = pltpu.get_barrier_semaphore()
    for d in range(1, n_e):
        pl.semaphore_signal(
            barrier, inc=1, device_id={"expert": lax.rem(me_e + d, n_e)}, device_id_type=MESH
        )
    for d in range(1, n_s):
        pl.semaphore_signal(
            barrier, inc=1, device_id={"seq": lax.rem(me_s + d, n_s)}, device_id_type=MESH
        )

    loads = {}
    for i, (name, src, dst) in enumerate(
        (
            ("tokens", tokens_h, tokens_v),
            ("norm_in", norm_in_h, norm_in_v),
            ("picks", picks_h, picks_v),
            ("queries", queries_h, q_v.at[me_s]),
            ("w_in", w_in_h.at[0], w_in_v),
            ("w_out", w_out_h.at[0], w_out_v),
            ("gates", gates_h, gates_v),
            ("counts", counts_h, counts_v),
            ("norm_out", norm_out_h, norm_out_v),
            ("w_key", w_key_h, w_key_v),
            ("w_value", w_value_h, w_value_v),
            ("w_proj", w_proj_h, w_proj_v),
        )
    ):
        loads[name] = pltpu.make_async_copy(src, dst, load_sem.at[i])
        loads[name].start()

    loads["tokens"].wait()
    loads["norm_in"].wait()
    loads["picks"].wait()
    normed = rms_norm(tokens_v[...].astype(F32), norm_in_v[...]).astype(BF16)
    pick_row = jnp.concatenate([picks_v[0, j : j + 1, :] for j in range(n_e)], axis=1)
    position = lax.broadcasted_iota(jnp.int32, (rows, n_e * slots), 0)
    chosen = jnp.where(position == pick_row, 1.0, 0.0).astype(BF16)
    a_copies = []
    piece = width // GATHER_PIECES
    for c in range(GATHER_PIECES):
        cols = slice(c * piece, (c + 1) * piece)
        outgoing = lax.dot_general(
            chosen, normed[:, cols], (((0,), (0,)), ((), ())), preferred_element_type=F32
        ).astype(BF16)
        send_a[:, :, cols] = outgoing.reshape(n_e, slots, piece)
        if c == 0:
            pl.semaphore_wait(barrier, n_e - 1 + n_s - 1)
        for d in range(1, n_e):
            off = d * upper + (n_e - d) * (1 - upper)
            to = lax.rem(me_e + off, n_e)
            copy = pltpu.make_async_remote_copy(
                src_ref=send_a.at[to, :, cols],
                dst_ref=recv_a.at[off, :, cols],
                send_sem=a_send.at[c, off],
                recv_sem=a_recv.at[c, off],
                device_id={"expert": to},
                device_id_type=MESH,
            )
            copy.start()
            a_copies.append(copy)
    loads["queries"].wait()
    q_copies = []
    for d in range(1, n_s):
        copy = pltpu.make_async_remote_copy(
            src_ref=q_v.at[me_s],
            dst_ref=q_v.at[me_s],
            send_sem=q_send.at[d],
            recv_sem=q_recv.at[d],
            device_id={"seq": lax.rem(me_s + d, n_s)},
            device_id_type=MESH,
        )
        copy.start()
        q_copies.append(copy)
    recv_a[0] = send_a[me_e]

    loads["gates"].wait()
    loads["counts"].wait()
    slot = lax.broadcasted_iota(jnp.int32, (1, slots), 1)
    gate_row = jnp.concatenate(
        [
            jnp.where(slot < counts_v[0:1, j : j + 1], gates_v[0, j : j + 1, :], 0.0)
            for j in range(n_e)
        ],
        axis=1,
    )
    high = gate_row.astype(BF16).astype(F32)
    middle = (gate_row - high).astype(BF16).astype(F32)
    low = gate_row - high - middle
    gate_three = jnp.concatenate([high, middle, low], axis=1)
    pick_three = jnp.concatenate([pick_row] * 3, axis=1)
    position_three = lax.broadcasted_iota(jnp.int32, (rows, 3 * n_e * slots), 0)
    combine = jnp.where(position_three == pick_three, gate_three, 0.0).astype(BF16)

    loads["w_in"].wait()
    for c in range(GATHER_PIECES):
        cols = slice(c * (width // GATHER_PIECES), (c + 1) * (width // GATHER_PIECES))
        for d in range(1, n_e):
            pltpu.make_async_remote_copy(
                src_ref=send_a.at[lax.rem(me_e + d, n_e), :, cols],
                dst_ref=recv_a.at[d, :, cols],
                send_sem=a_send.at[c, d],
                recv_sem=a_recv.at[c, d],
                device_id={"expert": lax.rem(me_e + d, n_e)},
                device_id_type=MESH,
            ).wait_recv()
    flat = recv_a[...].reshape(n_e * slots, width)
    hidden = gelu(jnp.dot(flat, w_in_v[...], preferred_element_type=F32)).astype(BF16)
    loads["w_out"].wait()
    b_copies = []
    piece = width // RETURN_PIECES
    for c in range(RETURN_PIECES):
        cols = slice(c * piece, (c + 1) * piece)
        result = jnp.dot(hidden, w_out_v[:, cols], preferred_element_type=F32).astype(BF16)
        send_b[:, :, cols] = result.reshape(n_e, slots, piece)
        for d in range(1, n_e):
            off = d * (1 - upper) + (n_e - d) * upper
            copy = pltpu.make_async_remote_copy(
                src_ref=send_b.at[off, :, cols],
                dst_ref=recv_b.at[me_e, :, cols],
                send_sem=b_send.at[c, off],
                recv_sem=b_recv.at[c, off],
                device_id={"expert": lax.rem(me_e + n_e - off, n_e)},
                device_id_type=MESH,
            )
            copy.start()
            b_copies.append(copy)
    recv_b[me_e] = send_b[0]

    loads["norm_out"].wait()
    loads["w_key"].wait()
    loads["w_value"].wait()
    for c in range(RETURN_PIECES):
        cols = slice(c * piece, (c + 1) * piece)
        for d in range(1, n_e):
            pltpu.make_async_remote_copy(
                src_ref=send_b.at[d, :, cols],
                dst_ref=recv_b.at[lax.rem(me_e + d, n_e), :, cols],
                send_sem=b_send.at[c, d],
                recv_sem=b_recv.at[c, d],
                device_id={"expert": lax.rem(me_e + n_e - d, n_e)},
                device_id_type=MESH,
            ).wait_recv()
    returned = recv_b[...].reshape(n_e * slots, width)
    expert_sum = jnp.dot(
        combine, jnp.concatenate([returned] * 3, axis=0), preferred_element_type=F32
    )
    mixed = tokens_v[...].astype(F32) + expert_sum
    encoded = rms_norm(mixed, norm_out_v[...]).astype(BF16)
    enc_v[...] = encoded
    keys = jnp.dot(encoded, w_key_v[...], preferred_element_type=F32).astype(BF16)
    values = jnp.dot(encoded, w_value_v[...], preferred_element_type=F32).astype(BF16)

    for d in range(1, n_s):
        pltpu.make_async_remote_copy(
            src_ref=q_v.at[me_s],
            dst_ref=q_v.at[lax.rem(me_s + n_s - d, n_s)],
            send_sem=q_send.at[d],
            recv_sem=q_recv.at[d],
            device_id={"seq": lax.rem(me_s + d, n_s)},
            device_id_type=MESH,
        ).wait_recv()
    all_rows = n_s * dec_rows
    queries = q_v[...].reshape(all_rows, q_width)
    slab = min(256, q_width)
    group = slab // head
    lane_head = lax.broadcasted_iota(jnp.int32, (1, slab), 1) // head
    lanes = part_v.shape[2] - q_width
    stat_lane = lax.broadcasted_iota(jnp.int32, (1, lanes), 1)
    stats = jnp.zeros((all_rows, lanes), F32)
    p_copies = []
    groups = q_width // slab
    for g in range(groups):
        cols = slice(g * slab, (g + 1) * slab)
        stacked = jnp.concatenate(
            [
                queries[:, cols] * jnp.where(lane_head == h, 1.0, 0.0).astype(BF16)
                for h in range(group)
            ],
            axis=0,
        )
        scores = lax.dot_general(
            stacked, keys[:, cols], (((1,), (1,)), ((), ())), preferred_element_type=F32
        ) * (head**-0.5)
        row_max = jnp.max(scores, axis=1, keepdims=True)
        weights = jnp.exp(scores - row_max)
        row_total = jnp.sum(weights, axis=1, keepdims=True)
        product = jnp.dot(weights.astype(BF16), values[:, cols], preferred_element_type=F32)
        joined = product[:all_rows]
        for h in range(group):
            span = slice(h * all_rows, (h + 1) * all_rows)
            if h:
                joined = jnp.where(lane_head == h, product[span], joined)
            at = g * group + h
            stats = jnp.where(stat_lane == at, row_max[span], stats)
            stats = jnp.where(stat_lane == HEADS + at, row_total[span], stats)
        part_v[:, :, cols] = joined.astype(BF16).reshape(n_s, dec_rows, slab)
        if g == groups - 1:
            high = stats.astype(BF16).astype(F32)
            middle = (stats - high).astype(BF16).astype(F32)
            low = stats - high - middle
            packed = high + pltpu.roll(middle, 2 * HEADS, 1) + pltpu.roll(low, 4 * HEADS, 1)
            part_v[:, :, q_width:] = packed.astype(BF16).reshape(n_s, dec_rows, lanes)
    for d in range(1, n_s):
        to = lax.rem(me_s + d, n_s)
        copy = pltpu.make_async_remote_copy(
            src_ref=part_v.at[to],
            dst_ref=part_r.at[d],
            send_sem=p_send.at[d],
            recv_sem=p_recv.at[d],
            device_id={"seq": to},
            device_id_type=MESH,
        )
        copy.start()
        p_copies.append(copy)
    part_r[0] = part_v[me_s]
    for copy in p_copies:
        copy.wait_recv()
    for copy in a_copies + b_copies + q_copies + p_copies:
        copy.wait_send()
    loads["w_proj"].wait()


def finish(
    enc_v, part_v, w_proj_v, encoded_h, dec_h, dec_v, store_sem
):
    enc_store = pltpu.make_async_copy(enc_v, encoded_h, store_sem.at[0])
    enc_store.start()
    n_s, dec_rows, _ = part_v.shape
    q_width = w_proj_v.shape[0]
    head = q_width // HEADS
    part = [part_v[d, :, :q_width].astype(F32) for d in range(n_s)]
    stat = []
    for d in range(n_s):
        packed = part_v[d, :, q_width:].astype(F32)
        lanes = packed.shape[1]
        stat.append(
            packed
            + pltpu.roll(packed, lanes - 2 * HEADS, 1)
            + pltpu.roll(packed, lanes - 4 * HEADS, 1)
        )
    top = functools.reduce(jnp.maximum, stat)
    factor = [jnp.exp(s - top)[:, :HEADS] for s in stat]
    total = sum(f * s[:, HEADS : 2 * HEADS] for f, s in zip(factor, stat))
    lane = lax.broadcasted_iota(jnp.int32, (1, q_width), 1) // head
    summed = jnp.zeros((dec_rows, q_width), F32)
    for f, p in zip(factor, part):
        scale = f / total
        spread = jnp.zeros((dec_rows, q_width), F32)
        for h in range(HEADS):
            spread = jnp.where(lane == h, scale[:, h : h + 1], spread)
        summed = summed + spread * p
    dec_v[...] = jnp.dot(
        summed.astype(BF16), w_proj_v[...], preferred_element_type=F32
    ).astype(BF16)
    dec_store = pltpu.make_async_copy(dec_v, dec_h, store_sem.at[1])
    dec_store.start()
    enc_store.wait()
    dec_store.wait()


def local(
    n_e,
    n_s,
    tokens,
    picks,
    gates,
    counts,
    norm_in,
    norm_out,
    w_in,
    w_out,
    w_key,
    w_value,
    queries,
    w_proj,
):
    rows, width = tokens.shape
    slots = picks.shape[2]
    hidden = w_in.shape[2]
    dec_rows, q_width = queries.shape
    lanes = 128 * pl.cdiv(6 * HEADS, 128)
    anywhere = pl.BlockSpec(memory_space=pl.ANY)
    dma = pltpu.SemaphoreType.DMA
    vmem = pl.BlockSpec(memory_space=pltpu.VMEM)
    room = 2 * (rows * width + n_s * dec_rows * (q_width + lanes) + q_width * width)
    encoded, part, w_proj_near = pl.pallas_call(
        functools.partial(kernel, n_e, n_s),
        out_shape=(
            pltpu.VMEM((rows, width), BF16),
            pltpu.VMEM((n_s, dec_rows, q_width + lanes), BF16),
            pltpu.VMEM((q_width, width), BF16),
        ),
        in_specs=[anywhere] * 12,
        out_specs=(vmem, vmem, vmem),
        scratch_shapes=[
            pltpu.VMEM((rows, width), BF16),
            pltpu.VMEM(picks.shape, jnp.int32),
            pltpu.VMEM(gates.shape, F32),
            pltpu.VMEM(counts.shape, jnp.int32),
            pltpu.VMEM((1, width), F32),
            pltpu.VMEM((1, width), F32),
            pltpu.VMEM((width, hidden), BF16),
            pltpu.VMEM((hidden, width), BF16),
            pltpu.VMEM((width, q_width), BF16),
            pltpu.VMEM((width, q_width), BF16),
            pltpu.VMEM((n_s, dec_rows, q_width), BF16),
            pltpu.VMEM((n_e, slots, width), BF16),
            pltpu.VMEM((n_e, slots, width), BF16),
            pltpu.VMEM((n_e, slots, width), BF16),
            pltpu.VMEM((n_e, slots, width), BF16),
            pltpu.VMEM((n_s, dec_rows, q_width + lanes), BF16),
            dma((12,)),
            dma((GATHER_PIECES, n_e)),
            dma((GATHER_PIECES, n_e)),
            dma((RETURN_PIECES, n_e)),
            dma((RETURN_PIECES, n_e)),
            dma((n_s,)),
            dma((n_s,)),
            dma((n_s,)),
            dma((n_s,)),
        ],
        compiler_params=pltpu.CompilerParams(
            collective_id=0, has_side_effects=True, vmem_limit_bytes=VMEM_BYTES - room
        ),
    )(
        tokens,
        picks,
        gates,
        counts,
        norm_in.reshape(1, -1),
        norm_out.reshape(1, -1),
        w_in,
        w_out,
        w_key,
        w_value,
        queries,
        w_proj,
    )
    return pl.pallas_call(
        finish,
        out_shape=(
            jax.ShapeDtypeStruct((rows, width), BF16),
            jax.ShapeDtypeStruct((dec_rows, width), BF16),
        ),
        in_specs=[vmem] * 3,
        out_specs=(anywhere, anywhere),
        scratch_shapes=[pltpu.VMEM((dec_rows, width), BF16), dma((2,))],
        compiler_params=pltpu.CompilerParams(vmem_limit_bytes=8 * 2**20),
    )(encoded, part, w_proj_near)


def solution(mesh):
    in_specs = (
        P(("dp", "expert", "seq"), None),
        P(("dp", "expert", "seq"), None, None),
        P(("dp", "expert", "seq"), None, None),
        P(("dp", "expert", "seq"), None),
        P(),
        P(),
        P("expert", None, None),
        P("expert", None, None),
        P(),
        P(),
        P(("dp", "expert", "seq"), None),
        P(),
    )
    out_specs = (P(("dp", "expert", "seq"), None), P(("dp", "expert", "seq"), None))
    body = functools.partial(local, mesh.shape["expert"], mesh.shape["seq"])
    return jax.shard_map(body, mesh=mesh, in_specs=in_specs, out_specs=out_specs, check_vma=False)
```

profile of v0, /device:TPU:0, one launch (start us, length us, event | category | flops | bytes accessed | tf_op | source)
XLA Modules:
  0.0 21.4 jit_solution(3138432610193475253)
XLA Ops:
  0.6 19.4 %shard_map.131 = (bf16[128,1024]{1,0:T(8,128)(2,1)S(1)}, bf16[4,32,640]{2,1,0:T(8,128)(2,1)S(1)}, bf16[512,1024]{1,0:T(8,128)(2,1)S(1)}) custom-call(bf16[128,1024]{1,0:T(8,128)(2,1)} %tokens_h.1, s32[1,4,16]{2,1,0:T(4,128)} %picks_h.1, f32[1,4,16]{2,1,0:T(4,128)} %gates_h.1, s32[1,4]{1,0:T(1,128)} %counts_h.1, f32[1,1024]{1,0:T(1,128)} %bitcast.2, ...), custom_call_target="tpu_custom_call" | custom-call | tf_op jit(solution)/shard_map/pallas_call | solution.py:367
  20.1 1.3 %shard_map.132 = (bf16[128,1024]{1,0:T(8,128)(2,1)}, bf16[32,1024]{1,0:T(8,128)(2,1)}) custom-call(bf16[128,1024]{1,0:T(8,128)(2,1)S(1)} %get-tuple-element.5.enc_v, bf16[4,32,640]{2,1,0:T(8,128)(2,1)S(1)} %get-tuple-element.6.part_v, bf16[512,1024]{1,0:T(8,128)(2,1)S(1)} %get-tuple-element.7.w_proj_v), custom_call_target="tpu_custom_call" | custom-call | tf_op jit(solution)/shard_map/pallas_call | solution.py:420
where the time goes:
time: 21.5 us; the launch traced here: 21.4 us
  Pallas kernels  20.7 us (96%)
  between operations  0.64 us (3%)
    pallas_call x1, Pallas kernels, local(): pl.pallas_call(functools.partial(kernel, n_e, n_s), out_shape=(pltpu.VMEM...  19.4 us
    pallas_call x1, Pallas kernels, local(): pl.pallas_call(finish, out_shape=(jax.ShapeDtypeStruct((rows, width), BF1...  1.3 us

commit v1 on v0

v1 whole, which is shorter than its diff:
```python
import functools

import jax
import jax.numpy as jnp
from jax import lax
from jax.experimental import pallas as pl
from jax.experimental.pallas import tpu as pltpu
from jax.sharding import PartitionSpec as P

HEADS = 8
EPSILON = 1e-06
VMEM_BYTES = 67043328
MESH = pl.DeviceIdType.MESH
F32 = jnp.float32
BF16 = jnp.bfloat16


def rms_norm(values, gain):
    mean_square = jnp.mean(values * values, axis=-1, keepdims=True)
    return values * lax.rsqrt(mean_square + EPSILON) * gain


def gelu(v):
    return 0.5 * v * (1.0 + jnp.tanh(0.7978845608028654 * (v + 0.044715 * v * v * v)))


def peer(n, at, r):
    upper = (2 * at) // n
    down = n - 1 - r
    return upper * (r + (r + n - at) // n) + (1 - upper) * (down - (at + n - down) // n)


def rank(n, at, other):
    upper = (2 * at) // n
    above = (other + n - 1 - at) // n
    below = (at + n - 1 - other) // n
    return upper * (other - above) + (1 - upper) * (n - 1 - other - below)


def kernel(
    n_e,
    n_s,
    tokens_h,
    picks_h,
    gates_h,
    counts_h,
    norm_in_h,
    norm_out_h,
    w_in_h,
    w_out_h,
    w_key_h,
    w_value_h,
    queries_h,
    w_proj_h,
    enc_v,
    dec_v,
    tokens_v,
    picks_v,
    gates_v,
    counts_v,
    norm_in_v,
    norm_out_v,
    w_in_v,
    w_out_v,
    w_key_v,
    w_value_v,
    w_proj_v,
    q_v,
    send_a,
    recv_a,
    send_b,
    recv_b,
    part_v,
    part_r,
    stat_v,
    stat_r,
    load_sem,
    a_send,
    a_recv,
    b_send,
    b_recv,
    q_send,
    q_recv,
    p_send,
    p_recv,
    t_send,
    t_recv,
):
    me_e = lax.axis_index("expert")
    me_s = lax.axis_index("seq")
    helper = lax.rem(me_s, 2)
    rows, width = tokens_v.shape
    slots = send_a.shape[1]
    dec_rows = q_v.shape[1]
    q_width = q_v.shape[2]
    head = q_width // HEADS
    own, far, extra = n_e - 2, n_e - 1, n_e

    loads = {}
    for i, (name, src, dst) in enumerate(
        (
            ("tokens", tokens_h, tokens_v),
            ("norm_in", norm_in_h, norm_in_v),
            ("picks", picks_h, picks_v),
            ("queries", queries_h, q_v.at[me_s]),
            ("w_in", w_in_h.at[0], w_in_v),
            ("w_out", w_out_h.at[0], w_out_v),
            ("gates", gates_h, gates_v),
            ("counts", counts_h, counts_v),
            ("norm_out", norm_out_h, norm_out_v),
            ("w_key", w_key_h, w_key_v),
            ("w_value", w_value_h, w_value_v),
            ("w_proj", w_proj_h, w_proj_v),
        )
    ):
        loads[name] = pltpu.make_async_copy(src, dst, load_sem.at[i])
    loads["tokens"].start()

    barrier = pltpu.get_barrier_semaphore()

    def greet(e, s):
        pl.semaphore_signal(
            barrier, inc=1, device_id={"expert": e, "seq": s}, device_id_type=MESH
        )

    @pl.when(helper == 1)
    def _():
        greet(peer(n_e, me_e, 0), me_s - 1)
        greet(peer(n_e, me_e, 0), me_s)

    for r in range(1, n_e - 1):
        greet(peer(n_e, me_e, r), me_s)
    for d in range(1, n_s):
        greet(me_e, lax.rem(me_s + d, n_s))
    for name in loads:
        if name != "tokens":
            loads[name].start()

    def copy_a(r):
        to = peer(n_e, me_e, r)
        place = rank(n_e, to, me_e)
        first = (n_e - place) // n_e
        aside = first * (1 - helper)
        slot = (1 - first) * (place - 1) + first * far + aside
        return pltpu.make_async_remote_copy(
            src_ref=send_a.at[to],
            dst_ref=recv_a.at[slot],
            send_sem=a_send.at[r],
            recv_sem=a_recv.at[slot],
            device_id={"expert": to, "seq": me_s + aside},
            device_id_type=MESH,
        )

    def arrive_a(slot):
        pltpu.make_async_remote_copy(
            src_ref=send_a.at[0],
            dst_ref=recv_a.at[slot],
            send_sem=a_send.at[0],
            recv_sem=a_recv.at[slot],
            device_id={"expert": peer(n_e, me_e, 0), "seq": me_s},
            device_id_type=MESH,
        ).wait_recv()

    def copy_b(slot):
        r = 0 if slot >= far else slot + 1
        aside = 1 if slot == extra else 0
        return pltpu.make_async_remote_copy(
            src_ref=send_b.at[slot],
            dst_ref=recv_b.at[me_e],
            send_sem=b_send.at[slot],
            recv_sem=b_recv.at[me_e],
            device_id={"expert": peer(n_e, me_e, r), "seq": me_s - aside},
            device_id_type=MESH,
        )

    def arrive_b(r):
        at = peer(n_e, me_e, r)
        pltpu.make_async_remote_copy(
            src_ref=send_b.at[0],
            dst_ref=recv_b.at[at],
            send_sem=b_send.at[0],
            recv_sem=b_recv.at[at],
            device_id={"expert": at, "seq": me_s},
            device_id_type=MESH,
        ).wait_recv()

    def copy_q(d, arriving=False):
        at = lax.rem(me_s + n_s - d, n_s) if arriving else me_s
        return pltpu.make_async_remote_copy(
            src_ref=q_v.at[me_s],
            dst_ref=q_v.at[at],
            send_sem=q_send.at[d],
            recv_sem=q_recv.at[d],
            device_id={"expert": me_e, "seq": lax.rem(me_s + d, n_s)},
            device_id_type=MESH,
        )

    def copy_p(d):
        to = lax.rem(me_s + d, n_s)
        return pltpu.make_async_remote_copy(
            src_ref=part_v.at[to],
            dst_ref=part_r.at[d],
            send_sem=p_send.at[d],
            recv_sem=p_recv.at[d],
            device_id={"expert": me_e, "seq": to},
            device_id_type=MESH,
        )

    def copy_t(d):
        to = lax.rem(me_s + d, n_s)
        return pltpu.make_async_remote_copy(
            src_ref=stat_v.at[to],
            dst_ref=stat_r.at[d],
            send_sem=t_send.at[d],
            recv_sem=t_recv.at[d],
            device_id={"expert": me_e, "seq": to},
            device_id_type=MESH,
        )

    loads["tokens"].wait()
    loads["norm_in"].wait()
    loads["picks"].wait()
    normed = rms_norm(tokens_v[...].astype(F32), norm_in_v[...]).astype(BF16)
    pick_row = jnp.concatenate([picks_v[0, j : j + 1, :] for j in range(n_e)], axis=1)
    position = lax.broadcasted_iota(jnp.int32, (rows, n_e * slots), 0)
    chosen = jnp.where(position == pick_row, 1.0, 0.0).astype(BF16)
    send_a[...] = (
        lax.dot_general(chosen, normed, (((0,), (0,)), ((), ())), preferred_element_type=F32)
        .astype(BF16)
        .reshape(n_e, slots, width)
    )
    pl.semaphore_wait(barrier, n_e - 1 + n_s - 1)
    for r in range(n_e - 1):
        copy_a(r).start()
    loads["queries"].wait()
    for d in range(1, n_s):
        copy_q(d).start()
    recv_a[own] = send_a[me_e]

    loads["gates"].wait()
    loads["counts"].wait()
    slot_lane = lax.broadcasted_iota(jnp.int32, (1, slots), 1)
    gate_row = jnp.concatenate(
        [
            jnp.where(slot_lane < counts_v[0:1, j : j + 1], gates_v[0, j : j + 1, :], 0.0)
            for j in range(n_e)
        ],
        axis=1,
    )
    high = gate_row.astype(BF16).astype(F32)
    middle = (gate_row - high).astype(BF16).astype(F32)
    low = gate_row - high - middle
    gate_three = jnp.concatenate([high, middle, low], axis=1)
    pick_three = jnp.concatenate([pick_row] * 3, axis=1)
    position_three = lax.broadcasted_iota(jnp.int32, (rows, 3 * n_e * slots), 0)
    combine = jnp.where(position_three == pick_three, gate_three, 0.0).astype(BF16)

    def feed(first, many):
        flat = recv_a[first : first + many].reshape(many * slots, width)
        hidden = gelu(jnp.dot(flat, w_in_v[...], preferred_element_type=F32)).astype(BF16)
        result = jnp.dot(hidden, w_out_v[...], preferred_element_type=F32).astype(BF16)
        send_b[first : first + many] = result.reshape(many, slots, width)

    loads["w_in"].wait()
    loads["w_out"].wait()
    for slot in range(own):
        arrive_a(slot)
    feed(0, own + 1)
    for slot in range(own):
        copy_b(slot).start()
    recv_b[me_e] = send_b[own]

    @pl.when(helper == 1)
    def _():
        arrive_a(far)
        arrive_a(extra)
        feed(far, 2)
        copy_b(extra).start()
        copy_b(far).start()

    loads["norm_out"].wait()
    loads["w_key"].wait()
    loads["w_value"].wait()
    for d in range(1, n_s):
        copy_q(d, True).wait_recv()
    all_rows = n_s * dec_rows
    queries = q_v[...].reshape(all_rows, q_width)
    for r in range(n_e - 1):
        arrive_b(n_e - 2 - r)
    returned = recv_b[...].reshape(n_e * slots, width)
    expert_sum = jnp.dot(
        combine, jnp.concatenate([returned] * 3, axis=0), preferred_element_type=F32
    )
    mixed = tokens_v[...].astype(F32) + expert_sum
    encoded = rms_norm(mixed, norm_out_v[...]).astype(BF16)
    enc_v[...] = encoded
    keys = jnp.dot(encoded, w_key_v[...], preferred_element_type=F32).astype(BF16)
    values = jnp.dot(encoded, w_value_v[...], preferred_element_type=F32).astype(BF16)

    slab = min(256, q_width)
    groups = q_width // slab
    group = slab // head
    lanes = stat_v.shape[2]
    lane_head = lax.broadcasted_iota(jnp.int32, (1, slab), 1) // head
    stat_lane = lax.broadcasted_iota(jnp.int32, (1, lanes), 1)
    bands = dec_rows // 8
    tops, totals = [], []
    for g in range(groups):
        cols = slice(g * slab, (g + 1) * slab)
        only = [jnp.where(lane_head == h, 1.0, 0.0).astype(BF16) for h in range(group)]
        key_heads = jnp.concatenate([keys[:, cols] * m for m in only], axis=0)
        value_heads = jnp.concatenate([values[:, cols] * m for m in only], axis=0)
        scores = lax.dot_general(
            queries[:, cols], key_heads, (((1,), (1,)), ((), ())), preferred_element_type=F32
        ) * (head**-0.5)
        weights = []
        for h in range(group):
            span = scores[:, h * rows : (h + 1) * rows]
            row_max = jnp.max(span, axis=1, keepdims=True)
            weight = jnp.exp(span - row_max)
            tops.append(row_max)
            totals.append(jnp.sum(weight, axis=1, keepdims=True))
            weights.append(weight.astype(BF16))
        product = jnp.dot(
            jnp.concatenate(weights, axis=1), value_heads, preferred_element_type=F32
        )
        part_v[:, :, cols] = product.astype(BF16).reshape(n_s, dec_rows, slab)
    for s in range(n_s):
        packed = jnp.zeros((8, lanes), F32)
        for band in range(bands):
            at = s * dec_rows + band * 8
            piece = jnp.zeros((8, lanes), F32)
            for h in range(HEADS):
                lane = band * 2 * HEADS + h
                piece = jnp.where(stat_lane == lane, tops[h][at : at + 8], piece)
                piece = jnp.where(stat_lane == lane + HEADS, totals[h][at : at + 8], piece)
            packed = packed + piece
        stat_v[s] = packed
    for d in range(1, n_s):
        copy_t(d).start()
        copy_p(d).start()
    part_r[0] = part_v[me_s]
    stat_r[0] = stat_v[me_s]

    loads["w_proj"].wait()
    for d in range(1, n_s):
        copy_t(d).wait_recv()
    stat = []
    for d in range(n_s):
        packed = stat_r[d]
        stat.append(
            jnp.concatenate(
                [
                    pltpu.roll(packed, lanes - band * 2 * HEADS, 1) if band else packed
                    for band in range(bands)
                ],
                axis=0,
            )
        )
    top = functools.reduce(jnp.maximum, stat)
    factor = [jnp.exp(s - top)[:, :HEADS] for s in stat]
    total = sum(f * s[:, HEADS : 2 * HEADS] for f, s in zip(factor, stat))
    for d in range(1, n_s):
        copy_p(d).wait_recv()
    answer = None
    for g in range(groups):
        cols = slice(g * slab, (g + 1) * slab)
        summed = jnp.zeros((dec_rows, slab), F32)
        for d in range(n_s):
            scale = factor[d] / total
            at = g * group
            spread = jnp.broadcast_to(scale[:, at : at + 1], (dec_rows, slab))
            for h in range(1, group):
                spread = jnp.where(lane_head == h, scale[:, at + h : at + h + 1], spread)
            summed = summed + spread * part_r[d, :, cols].astype(F32)
        term = jnp.dot(summed.astype(BF16), w_proj_v[cols], preferred_element_type=F32)
        answer = term if answer is None else answer + term
    dec_v[...] = answer.astype(BF16)

    for r in range(n_e - 1):
        copy_a(r).wait_send()
    for slot in range(own):
        copy_b(slot).wait_send()

    @pl.when(helper == 1)
    def _():
        copy_b(extra).wait_send()
        copy_b(far).wait_send()

    for d in range(1, n_s):
        copy_q(d).wait_send()
        copy_p(d).wait_send()
        copy_t(d).wait_send()


def finish(enc_v, dec_v, encoded_h, dec_h, store_sem):
    enc_store = pltpu.make_async_copy(enc_v, encoded_h, store_sem.at[0])
    dec_store = pltpu.make_async_copy(dec_v, dec_h, store_sem.at[1])
    enc_store.start()
    dec_store.start()
    enc_store.wait()
    dec_store.wait()


def local(
    n_e,
    n_s,
    tokens,
    picks,
    gates,
    counts,
    norm_in,
    norm_out,
    w_in,
    w_out,
    w_key,
    w_value,
    queries,
    w_proj,
):
    rows, width = tokens.shape
    slots = picks.shape[2]
    hidden = w_in.shape[2]
    dec_rows, q_width = queries.shape
    lanes = 128 * pl.cdiv((dec_rows // 8) * 2 * HEADS, 128)
    anywhere = pl.BlockSpec(memory_space=pl.ANY)
    dma = pltpu.SemaphoreType.DMA
    vmem = pl.BlockSpec(memory_space=pltpu.VMEM)
    room = 2 * (rows * width + dec_rows * width)
    encoded, dec = pl.pallas_call(
        functools.partial(kernel, n_e, n_s),
        out_shape=(
            pltpu.VMEM((rows, width), BF16),
            pltpu.VMEM((dec_rows, width), BF16),
        ),
        in_specs=[anywhere] * 12,
        out_specs=(vmem, vmem),
        scratch_shapes=[
            pltpu.VMEM((rows, width), BF16),
            pltpu.VMEM(picks.shape, jnp.int32),
            pltpu.VMEM(gates.shape, F32),
            pltpu.VMEM(counts.shape, jnp.int32),
            pltpu.VMEM((1, width), F32),
            pltpu.VMEM((1, width), F32),
            pltpu.VMEM((width, hidden), BF16),
            pltpu.VMEM((hidden, width), BF16),
            pltpu.VMEM((width, q_width), BF16),
            pltpu.VMEM((width, q_width), BF16),
            pltpu.VMEM((q_width, width), BF16),
            pltpu.VMEM((n_s, dec_rows, q_width), BF16),
            pltpu.VMEM((n_e, slots, width), BF16),
            pltpu.VMEM((n_e + 1, slots, width), BF16),
            pltpu.VMEM((n_e + 1, slots, width), BF16),
            pltpu.VMEM((n_e, slots, width), BF16),
            pltpu.VMEM((n_s, dec_rows, q_width), BF16),
            pltpu.VMEM((n_s, dec_rows, q_width), BF16),
            pltpu.VMEM((n_s, 8, lanes), F32),
            pltpu.VMEM((n_s, 8, lanes), F32),
            dma((12,)),
            dma((n_e - 1,)),
            dma((n_e + 1,)),
            dma((n_e + 1,)),
            dma((n_e,)),
            dma((n_s,)),
            dma((n_s,)),
            dma((n_s,)),
            dma((n_s,)),
            dma((n_s,)),
            dma((n_s,)),
        ],
        compiler_params=pltpu.CompilerParams(
            collective_id=0, has_side_effects=True, vmem_limit_bytes=VMEM_BYTES - room
        ),
    )(
        tokens,
        picks,
        gates,
        counts,
        norm_in.reshape(1, -1),
        norm_out.reshape(1, -1),
        w_in,
        w_out,
        w_key,
        w_value,
        queries,
        w_proj,
    )
    return pl.pallas_call(
        finish,
        out_shape=(
            jax.ShapeDtypeStruct((rows, width), BF16),
            jax.ShapeDtypeStruct((dec_rows, width), BF16),
        ),
        in_specs=[vmem] * 2,
        out_specs=(anywhere, anywhere),
        scratch_shapes=[dma((2,))],
        compiler_params=pltpu.CompilerParams(vmem_limit_bytes=8 * 2**20),
    )(encoded, dec)


def solution(mesh):
    in_specs = (
        P(("dp", "expert", "seq"), None),
        P(("dp", "expert", "seq"), None, None),
        P(("dp", "expert", "seq"), None, None),
        P(("dp", "expert", "seq"), None),
        P(),
        P(),
        P("expert", None, None),
        P("expert", None, None),
        P(),
        P(),
        P(("dp", "expert", "seq"), None),
        P(),
    )
    out_specs = (P(("dp", "expert", "seq"), None), P(("dp", "expert", "seq"), None))
    body = functools.partial(local, mesh.shape["expert"], mesh.shape["seq"])
    return jax.shard_map(body, mesh=mesh, in_specs=in_specs, out_specs=out_specs, check_vma=False)
```

time: 21.5 us -> 21 us (0.977)
  Pallas kernels: 20.7 us -> 20.2 us
    pallas_call x1, Pallas kernels: 1.3 us -> 0.74 us  [local(): pl.pallas_call(finish, out_shape=(jax.ShapeDtypeStruct((rows, width), BF1...]
where the time goes in v1:
time: 21 us; the launch traced here: 20.9 us
  Pallas kernels  20.2 us (96%)
  between operations  0.64 us (3%)
    pallas_call x1, Pallas kernels, local(): pl.pallas_call(functools.partial(kernel, n_e, n_s), out_shape=(pltpu.VMEM...  19.5 us
    pallas_call x1, Pallas kernels, local(): pl.pallas_call(finish, out_shape=(jax.ShapeDtypeStruct((rows, width), BF1...  0.74 us

profile of v1, /device:TPU:0, one launch (start us, length us, event | category | flops | bytes accessed | tf_op | source)
XLA Modules:
  0.0 20.9 jit_solution(10760629606954071234)
XLA Ops:
  0.6 19.5 %shard_map.131 = (bf16[128,1024]{1,0:T(8,128)(2,1)S(1)}, bf16[32,1024]{1,0:T(8,128)(2,1)S(1)}) custom-call(bf16[128,1024]{1,0:T(8,128)(2,1)} %tokens_h.1, s32[1,4,16]{2,1,0:T(4,128)} %picks_h.1, f32[1,4,16]{2,1,0:T(4,128)} %gates_h.1, s32[1,4]{1,0:T(1,128)} %counts_h.1, f32[1,1024]{1,0:T(1,128)} %bitcast.2, f32[1,1024]{1,0:T(1,128)} %bitcast.3, ...), custom_call_target="tpu_custom_call" | custom-call | tf_op jit(solution)/shard_map/pallas_call | solution.py:430
  20.1 0.7 %shard_map.132 = (bf16[128,1024]{1,0:T(8,128)(2,1)}, bf16[32,1024]{1,0:T(8,128)(2,1)}) custom-call(bf16[128,1024]{1,0:T(8,128)(2,1)S(1)} %get-tuple-element.4.enc_v, bf16[32,1024]{1,0:T(8,128)(2,1)S(1)} %get-tuple-element.5.dec_v), custom_call_target="tpu_custom_call" | custom-call | tf_op jit(solution)/shard_map/pallas_call | solution.py:488

commit v2 on v1

--- a/solution.py
+++ b/solution.py
@@ -25,15 +25,15 @@
 
 
 def peer(n, at, r):
-    upper = (2 * at) // n
+    upper = lax.div(2 * at, n)
     down = n - 1 - r
-    return upper * (r + (r + n - at) // n) + (1 - upper) * (down - (at + n - down) // n)
+    return upper * (r + lax.div(r + n - at, n)) + (1 - upper) * (down - lax.div(at + n - down, n))
 
 
 def rank(n, at, other):
-    upper = (2 * at) // n
-    above = (other + n - 1 - at) // n
-    below = (at + n - 1 - other) // n
+    upper = lax.div(2 * at, n)
+    above = lax.div(other + n - 1 - at, n)
+    below = lax.div(at + n - 1 - other, n)
     return upper * (other - above) + (1 - upper) * (n - 1 - other - below)
 
 
@@ -58,12 +58,10 @@
     picks_v,
     gates_v,
     counts_v,
-    norm_in_v,
-    norm_out_v,
+    norms_v,
     w_in_v,
     w_out_v,
-    w_key_v,
-    w_value_v,
+    w_kv_v,
     w_proj_v,
     q_v,
     send_a,
@@ -74,6 +72,7 @@
     part_r,
     stat_v,
     stat_r,
+    spread_v,
     load_sem,
     a_send,
     a_recv,
@@ -100,21 +99,32 @@
     for i, (name, src, dst) in enumerate(
         (
             ("tokens", tokens_h, tokens_v),
-            ("norm_in", norm_in_h, norm_in_v),
             ("picks", picks_h, picks_v),
             ("queries", queries_h, q_v.at[me_s]),
             ("w_in", w_in_h.at[0], w_in_v),
             ("w_out", w_out_h.at[0], w_out_v),
             ("gates", gates_h, gates_v),
             ("counts", counts_h, counts_v),
-            ("norm_out", norm_out_h, norm_out_v),
-            ("w_key", w_key_h, w_key_v),
-            ("w_value", w_value_h, w_value_v),
             ("w_proj", w_proj_h, w_proj_v),
         )
     ):
         loads[name] = pltpu.make_async_copy(src, dst, load_sem.at[i])
+    pairs = {}
+    for i, (name, parts, dst) in enumerate(
+        (("norms", (norm_in_h, norm_out_h), norms_v), ("w_kv", (w_key_h, w_value_h), w_kv_v))
+    ):
+        sem = load_sem.at[len(loads) + i]
+        pairs[name] = [
+            pltpu.make_async_copy(part, dst.at[k], sem) for k, part in enumerate(parts)
+        ]
+    both = {
+        name: pltpu.make_async_copy(dst, dst, load_sem.at[len(loads) + i])
+        for i, (name, dst) in enumerate((("norms", norms_v), ("w_kv", w_kv_v)))
+    }
     loads["tokens"].start()
+    loads["picks"].start()
+    for copy in pairs["norms"]:
+        copy.start()
 
     barrier = pltpu.get_barrier_semaphore()
 
@@ -132,95 +142,64 @@
         greet(peer(n_e, me_e, r), me_s)
     for d in range(1, n_s):
         greet(me_e, lax.rem(me_s + d, n_s))
-    for name in loads:
-        if name != "tokens":
-            loads[name].start()
+    for name in ("queries", "w_in", "w_out", "gates", "counts"):
+        loads[name].start()
+    for copy in pairs["w_kv"]:
+        copy.start()
+    loads["w_proj"].start()
+
+    def remote(src, dst, send, recv, e, s):
+        return pltpu.make_async_remote_copy(
+            src_ref=src,
+            dst_ref=dst,
+            send_sem=send,
+            recv_sem=recv,
+            device_id={"expert": e, "seq": s},
+            device_id_type=MESH,
+        )
 
     def copy_a(r):
         to = peer(n_e, me_e, r)
         place = rank(n_e, to, me_e)
-        first = (n_e - place) // n_e
+        first = lax.div(n_e - place, n_e)
         aside = first * (1 - helper)
         slot = (1 - first) * (place - 1) + first * far + aside
-        return pltpu.make_async_remote_copy(
-            src_ref=send_a.at[to],
-            dst_ref=recv_a.at[slot],
-            send_sem=a_send.at[r],
-            recv_sem=a_recv.at[slot],
-            device_id={"expert": to, "seq": me_s + aside},
-            device_id_type=MESH,
-        )
-
-    def arrive_a(slot):
-        pltpu.make_async_remote_copy(
-            src_ref=send_a.at[0],
-            dst_ref=recv_a.at[slot],
-            send_sem=a_send.at[0],
-            recv_sem=a_recv.at[slot],
-            device_id={"expert": peer(n_e, me_e, 0), "seq": me_s},
-            device_id_type=MESH,
-        ).wait_recv()
+        return remote(
+            send_a.at[to], recv_a.at[slot], a_send.at[0], a_recv.at[first + aside], to, me_s + aside
+        )
 
     def copy_b(slot):
-        r = 0 if slot >= far else slot + 1
         aside = 1 if slot == extra else 0
-        return pltpu.make_async_remote_copy(
-            src_ref=send_b.at[slot],
-            dst_ref=recv_b.at[me_e],
-            send_sem=b_send.at[slot],
-            recv_sem=b_recv.at[me_e],
-            device_id={"expert": peer(n_e, me_e, r), "seq": me_s - aside},
-            device_id_type=MESH,
-        )
-
-    def arrive_b(r):
-        at = peer(n_e, me_e, r)
-        pltpu.make_async_remote_copy(
-            src_ref=send_b.at[0],
-            dst_ref=recv_b.at[at],
-            send_sem=b_send.at[0],
-            recv_sem=b_recv.at[at],
-            device_id={"expert": at, "seq": me_s},
-            device_id_type=MESH,
-        ).wait_recv()
-
-    def copy_q(d, arriving=False):
-        at = lax.rem(me_s + n_s - d, n_s) if arriving else me_s
-        return pltpu.make_async_remote_copy(
-            src_ref=q_v.at[me_s],
-            dst_ref=q_v.at[at],
-            send_sem=q_send.at[d],
-            recv_sem=q_recv.at[d],
-            device_id={"expert": me_e, "seq": lax.rem(me_s + d, n_s)},
-            device_id_type=MESH,
-        )
+        return remote(
+            send_b.at[slot],
+            recv_b.at[me_e],
+            b_send.at[1 if slot >= far else 0],
+            b_recv.at[0],
+            peer(n_e, me_e, 0 if slot >= far else slot + 1),
+            me_s - aside,
+        )
+
+    def whole(ref, first, many, sem):
+        piece = ref.at[pl.ds(first, many)]
+        return pltpu.make_async_copy(piece, piece, sem)
+
+    def copy_q(d):
+        to = lax.rem(me_s + d, n_s)
+        return remote(q_v.at[me_s], q_v.at[me_s], q_send.at[0], q_recv.at[0], me_e, to)
 
     def copy_p(d):
         to = lax.rem(me_s + d, n_s)
-        return pltpu.make_async_remote_copy(
-            src_ref=part_v.at[to],
-            dst_ref=part_r.at[d],
-            send_sem=p_send.at[d],
-            recv_sem=p_recv.at[d],
-            device_id={"expert": me_e, "seq": to},
-            device_id_type=MESH,
-        )
+        return remote(part_v.at[to], part_r.at[d], p_send.at[0], p_recv.at[0], me_e, to)
 
     def copy_t(d):
         to = lax.rem(me_s + d, n_s)
-        return pltpu.make_async_remote_copy(
-            src_ref=stat_v.at[to],
-            dst_ref=stat_r.at[d],
-            send_sem=t_send.at[d],
-            recv_sem=t_recv.at[d],
-            device_id={"expert": me_e, "seq": to},
-            device_id_type=MESH,
-        )
-
+        return remote(stat_v.at[to], stat_r.at[d], t_send.at[0], t_recv.at[0], me_e, to)
+
+    a_copies = [copy_a(r) for r in range(n_e - 1)]
     loads["tokens"].wait()
-    loads["norm_in"].wait()
+    both["norms"].wait()
     loads["picks"].wait()
-    normed = rms_norm(tokens_v[...].astype(F32), norm_in_v[...]).astype(BF16)
+    normed = rms_norm(tokens_v[...].astype(F32), norms_v[0]).astype(BF16)
     pick_row = jnp.concatenate([picks_v[0, j : j + 1, :] for j in range(n_e)], axis=1)
     position = lax.broadcasted_iota(jnp.int32, (rows, n_e * slots), 0)
     chosen = jnp.where(position == pick_row, 1.0, 0.0).astype(BF16)
@@ -230,8 +209,8 @@
         .reshape(n_e, slots, width)
     )
     pl.semaphore_wait(barrier, n_e - 1 + n_s - 1)
-    for r in range(n_e - 1):
-        copy_a(r).start()
+    for copy in a_copies:
+        copy.start()
     loads["queries"].wait()
     for d in range(1, n_s):
         copy_q(d).start()
@@ -263,40 +242,34 @@
 
     loads["w_in"].wait()
     loads["w_out"].wait()
-    for slot in range(own):
-        arrive_a(slot)
-    feed(0, own + 1)
+    feed(own, 1)
+    recv_b[me_e] = send_b[own]
+    whole(recv_a, 0, own, a_recv.at[0]).wait()
+    feed(0, own)
     for slot in range(own):
         copy_b(slot).start()
-    recv_b[me_e] = send_b[own]
 
     @pl.when(helper == 1)
     def _():
-        arrive_a(far)
-        arrive_a(extra)
-        feed(far, 2)
+        whole(recv_a, far, 1, a_recv.at[1]).wait()
+        feed(far, 1)
+        copy_b(far).start()
+        whole(recv_a, extra, 1, a_recv.at[2]).wait()
+        feed(extra, 1)
         copy_b(extra).start()
-        copy_b(far).start()
-
-    loads["norm_out"].wait()
-    loads["w_key"].wait()
-    loads["w_value"].wait()
-    for d in range(1, n_s):
-        copy_q(d, True).wait_recv()
+
+    both["w_kv"].wait()
+    whole(q_v, 0, n_s - 1, q_recv.at[0]).wait()
     all_rows = n_s * dec_rows
     queries = q_v[...].reshape(all_rows, q_width)
-    for r in range(n_e - 1):
-        arrive_b(n_e - 2 - r)
+    whole(recv_b, 0, n_e - 1, b_recv.at[0]).wait()
     returned = recv_b[...].reshape(n_e * slots, width)
     expert_sum = jnp.dot(
         combine, jnp.concatenate([returned] * 3, axis=0), preferred_element_type=F32
     )
     mixed = tokens_v[...].astype(F32) + expert_sum
-    encoded = rms_norm(mixed, norm_out_v[...]).astype(BF16)
+    encoded = rms_norm(mixed, norms_v[1]).astype(BF16)
     enc_v[...] = encoded
-    keys = jnp.dot(encoded, w_key_v[...], preferred_element_type=F32).astype(BF16)
-    values = jnp.dot(encoded, w_value_v[...], preferred_element_type=F32).astype(BF16)
-
     slab = min(256, q_width)
     groups = q_width // slab
     group = slab // head
@@ -304,23 +277,30 @@
     lane_head = lax.broadcasted_iota(jnp.int32, (1, slab), 1) // head
     stat_lane = lax.broadcasted_iota(jnp.int32, (1, lanes), 1)
     bands = dec_rows // 8
+    only = [jnp.where(lane_head == h, 1.0, 0.0).astype(BF16) for h in range(group)]
+    slabs = [slice(g * slab, (g + 1) * slab) for g in range(groups)]
+    keys = jnp.dot(encoded, w_kv_v[0], preferred_element_type=F32).astype(BF16)
+    scores = []
+    for cols in slabs:
+        key_heads = jnp.concatenate([keys[:, cols] * m for m in only], axis=0)
+        scores.append(
+            lax.dot_general(
+                queries[:, cols], key_heads, (((1,), (1,)), ((), ())), preferred_element_type=F32
+            )
+            * (head**-0.5)
+        )
+    values = jnp.dot(encoded, w_kv_v[1], preferred_element_type=F32).astype(BF16)
     tops, totals = [], []
-    for g in range(groups):
-        cols = slice(g * slab, (g + 1) * slab)
-        only = [jnp.where(lane_head == h, 1.0, 0.0).astype(BF16) for h in range(group)]
-        key_heads = jnp.concatenate([keys[:, cols] * m for m in only], axis=0)
-        value_heads = jnp.concatenate([values[:, cols] * m for m in only], axis=0)
-        scores = lax.dot_general(
-            queries[:, cols], key_heads, (((1,), (1,)), ((), ())), preferred_element_type=F32
-        ) * (head**-0.5)
+    for cols, score in zip(slabs, scores):
         weights = []
         for h in range(group):
-            span = scores[:, h * rows : (h + 1) * rows]
+            span = score[:, h * rows : (h + 1) * rows]
             row_max = jnp.max(span, axis=1, keepdims=True)
             weight = jnp.exp(span - row_max)
             tops.append(row_max)
             totals.append(jnp.sum(weight, axis=1, keepdims=True))
             weights.append(weight.astype(BF16))
+        value_heads = jnp.concatenate([values[:, cols] * m for m in only], axis=0)
         product = jnp.dot(
             jnp.concatenate(weights, axis=1), value_heads, preferred_element_type=F32
         )
@@ -342,9 +322,16 @@
     part_r[0] = part_v[me_s]
     stat_r[0] = stat_v[me_s]
 
+    whole(send_a, 0, n_e - 1, a_send.at[0]).wait()
+    whole(send_b, 0, own, b_send.at[0]).wait()
+
+    @pl.when(helper == 1)
+    def _():
+        whole(send_b, far, 2, b_send.at[1]).wait()
+
+    whole(q_v, 0, n_s - 1, q_send.at[0]).wait()
     loads["w_proj"].wait()
-    for d in range(1, n_s):
-        copy_t(d).wait_recv()
+    whole(stat_r, 1, n_s - 1, t_recv.at[0]).wait()
     stat = []
     for d in range(n_s):
         packed = stat_r[d]
@@ -360,37 +347,21 @@
     top = functools.reduce(jnp.maximum, stat)
     factor = [jnp.exp(s - top)[:, :HEADS] for s in stat]
     total = sum(f * s[:, HEADS : 2 * HEADS] for f, s in zip(factor, stat))
-    for d in range(1, n_s):
-        copy_p(d).wait_recv()
-    answer = None
-    for g in range(groups):
-        cols = slice(g * slab, (g + 1) * slab)
-        summed = jnp.zeros((dec_rows, slab), F32)
-        for d in range(n_s):
-            scale = factor[d] / total
+    for d in range(n_s):
+        scale = factor[d] / total
+        for g, cols in enumerate(slabs):
             at = g * group
             spread = jnp.broadcast_to(scale[:, at : at + 1], (dec_rows, slab))
             for h in range(1, group):
                 spread = jnp.where(lane_head == h, scale[:, at + h : at + h + 1], spread)
-            summed = summed + spread * part_r[d, :, cols].astype(F32)
-        term = jnp.dot(summed.astype(BF16), w_proj_v[cols], preferred_element_type=F32)
-        answer = term if answer is None else answer + term
-    dec_v[...] = answer.astype(BF16)
-
-    for r in range(n_e - 1):
-        copy_a(r).wait_send()
-    for slot in range(own):
-        copy_b(slot).wait_send()
-
-    @pl.when(helper == 1)
-    def _():
-        copy_b(extra).wait_send()
-        copy_b(far).wait_send()
-
-    for d in range(1, n_s):
-        copy_q(d).wait_send()
-        copy_p(d).wait_send()
-        copy_t(d).wait_send()
+            spread_v[d, :, cols] = spread
+    whole(stat_v, 0, n_s - 1, t_send.at[0]).wait()
+    whole(part_v, 0, n_s - 1, p_send.at[0]).wait()
+    whole(part_r, 1, n_s - 1, p_recv.at[0]).wait()
+    summed = sum(spread_v[d] * part_r[d].astype(F32) for d in range(n_s))
+    dec_v[...] = jnp.dot(
+        summed.astype(BF16), w_proj_v[...], preferred_element_type=F32
+    ).astype(BF16)
 
 
 def finish(enc_v, dec_v, encoded_h, dec_h, store_sem):
@@ -440,12 +411,10 @@
             pltpu.VMEM(picks.shape, jnp.int32),
             pltpu.VMEM(gates.shape, F32),
             pltpu.VMEM(counts.shape, jnp.int32),
-            pltpu.VMEM((1, width), F32),
-            pltpu.VMEM((1, width), F32),
+            pltpu.VMEM((2, 1, width), F32),
             pltpu.VMEM((width, hidden), BF16),
             pltpu.VMEM((hidden, width), BF16),
-            pltpu.VMEM((width, q_width), BF16),
-            pltpu.VMEM((width, q_width), BF16),
+            pltpu.VMEM((2, width, q_width), BF16),
             pltpu.VMEM((q_width, width), BF16),
             pltpu.VMEM((n_s, dec_rows, q_width), BF16),
             pltpu.VMEM((n_e, slots, width), BF16),
@@ -456,17 +425,18 @@
             pltpu.VMEM((n_s, dec_rows, q_width), BF16),
             pltpu.VMEM((n_s, 8, lanes), F32),
             pltpu.VMEM((n_s, 8, lanes), F32),
-            dma((12,)),
-            dma((n_e - 1,)),
-            dma((n_e + 1,)),
-            dma((n_e + 1,)),
-            dma((n_e,)),
-            dma((n_s,)),
-            dma((n_s,)),
-            dma((n_s,)),
-            dma((n_s,)),
-            dma((n_s,)),
-            dma((n_s,)),
+            pltpu.VMEM((n_s, dec_rows, q_width), F32),
+            dma((10,)),
+            dma((1,)),
+            dma((3,)),
+            dma((2,)),
+            dma((1,)),
+            dma((1,)),
+            dma((1,)),
+            dma((1,)),
+            dma((1,)),
+            dma((1,)),
+            dma((1,)),
         ],
         compiler_params=pltpu.CompilerParams(
             collective_id=0, has_side_effects=True, vmem_limit_bytes=VMEM_BYTES - room

time: 21 us -> 20.1 us (0.957)
  Pallas kernels: 20.2 us -> 19.3 us
    pallas_call x1, Pallas kernels: 19.5 us -> 18.6 us  [local(): pl.pallas_call(functools.partial(kernel, n_e, n_s), out_shape=(pltpu.VMEM...]
where the time goes in v2:
time: 20.1 us; the launch traced here: 20 us
  Pallas kernels  19.3 us (96%)
  between operations  0.64 us (3%)
    pallas_call x1, Pallas kernels, local(): pl.pallas_call(functools.partial(kernel, n_e, n_s), out_shape=(pltpu.VMEM...  18.6 us
    pallas_call x1, Pallas kernels, local(): pl.pallas_call(finish, out_shape=(jax.ShapeDtypeStruct((rows, width), BF1...  0.74 us

profile of v2, /device:TPU:0, one launch (start us, length us, event | category | flops | bytes accessed | tf_op | source)
XLA Modules:
  0.0 20.0 jit_solution(10650846733246500392)
XLA Ops:
  0.6 18.6 %shard_map.131 = (bf16[128,1024]{1,0:T(8,128)(2,1)S(1)}, bf16[32,1024]{1,0:T(8,128)(2,1)S(1)}) custom-call(bf16[128,1024]{1,0:T(8,128)(2,1)} %tokens_h.1, s32[1,4,16]{2,1,0:T(4,128)} %picks_h.1, f32[1,4,16]{2,1,0:T(4,128)} %gates_h.1, s32[1,4]{1,0:T(1,128)} %counts_h.1, f32[1,1024]{1,0:T(1,128)} %bitcast.2, f32[1,1024]{1,0:T(1,128)} %bitcast.3, ...), custom_call_target="tpu_custom_call" | custom-call | tf_op jit(solution)/shard_map/pallas_call | solution.py:401
  19.2 0.7 %shard_map.132 = (bf16[128,1024]{1,0:T(8,128)(2,1)}, bf16[32,1024]{1,0:T(8,128)(2,1)}) custom-call(bf16[128,1024]{1,0:T(8,128)(2,1)S(1)} %get-tuple-element.4.enc_v, bf16[32,1024]{1,0:T(8,128)(2,1)S(1)} %get-tuple-element.5.dec_v), custom_call_target="tpu_custom_call" | custom-call | tf_op jit(solution)/shard_map/pallas_call | solution.py:458

commit v3 on v2

--- a/solution.py
+++ b/solution.py
@@ -165,7 +165,7 @@
         aside = first * (1 - helper)
         slot = (1 - first) * (place - 1) + first * far + aside
         return remote(
-            send_a.at[to], recv_a.at[slot], a_send.at[0], a_recv.at[first + aside], to, me_s + aside
+            send_a.at[to], recv_a.at[slot], a_send.at[0], a_recv.at[slot], to, me_s + aside
         )
 
     def copy_b(slot):
@@ -234,27 +234,61 @@
     position_three = lax.broadcasted_iota(jnp.int32, (rows, 3 * n_e * slots), 0)
     combine = jnp.where(position_three == pick_three, gate_three, 0.0).astype(BF16)
 
-    def feed(first, many):
+    def feed(first, many, second=0, more=0):
         flat = recv_a[first : first + many].reshape(many * slots, width)
+        if more:
+            rest = recv_a[second : second + more].reshape(more * slots, width)
+            flat = jnp.concatenate([flat, rest], axis=0)
         hidden = gelu(jnp.dot(flat, w_in_v[...], preferred_element_type=F32)).astype(BF16)
         result = jnp.dot(hidden, w_out_v[...], preferred_element_type=F32).astype(BF16)
-        send_b[first : first + many] = result.reshape(many, slots, width)
+        send_b[first : first + many] = result[: many * slots].reshape(many, slots, width)
+        if more:
+            send_b[second : second + more] = result[many * slots :].reshape(more, slots, width)
 
     loads["w_in"].wait()
     loads["w_out"].wait()
     feed(own, 1)
     recv_b[me_e] = send_b[own]
-    whole(recv_a, 0, own, a_recv.at[0]).wait()
-    feed(0, own)
-    for slot in range(own):
-        copy_b(slot).start()
-
-    @pl.when(helper == 1)
+    near = [whole(recv_a, slot, 1, a_recv.at[slot]) for slot in range(own)]
+    far_own = whole(recv_a, far, 1, a_recv.at[far])
+    far_aside = whole(recv_a, extra, 1, a_recv.at[extra])
+    together = helper * lax.div(2 * me_e, n_e) * (1 - lax.div(me_e + 1, n_e))
+
+    @pl.when(together == 1)
     def _():
-        whole(recv_a, far, 1, a_recv.at[1]).wait()
+        for copy in near:
+            copy.wait()
+        far_own.wait()
+        feed(0, own, far, 1)
+        copy_b(far).start()
+        for slot in range(own):
+            copy_b(slot).start()
+        far_aside.wait()
+        feed(extra, 1)
+        copy_b(extra).start()
+
+    @pl.when(helper == 0)
+    def _():
+        for slot in reversed(range(own)):
+            near[slot].wait()
+            feed(slot, 1)
+            copy_b(slot).start()
+
+    @pl.when(helper - together == 1)
+    def _():
+        for copy in near:
+            copy.wait()
+        feed(0, own)
+        for slot in range(own):
+            copy_b(slot).start()
+
+
+    @pl.when(helper - together == 1)
+    def _():
+        far_own.wait()
         feed(far, 1)
         copy_b(far).start()
-        whole(recv_a, extra, 1, a_recv.at[2]).wait()
+        far_aside.wait()
         feed(extra, 1)
         copy_b(extra).start()
 
@@ -428,7 +462,7 @@
             pltpu.VMEM((n_s, dec_rows, q_width), F32),
             dma((10,)),
             dma((1,)),
-            dma((3,)),
+            dma((n_e + 1,)),
             dma((2,)),
             dma((1,)),
             dma((1,)),

time: 20.1 us -> 19.9 us (0.990)
  no operation moved by 1% of the time
where the time goes in v3:
time: 19.9 us; the launch traced here: 19.8 us
  Pallas kernels  19.1 us (96%)
  between operations  0.64 us (3%)
    pallas_call x1, Pallas kernels, local(): pl.pallas_call(functools.partial(kernel, n_e, n_s), out_shape=(pltpu.VMEM...  18.4 us
    pallas_call x1, Pallas kernels, local(): pl.pallas_call(finish, out_shape=(jax.ShapeDtypeStruct((rows, width), BF1...  0.74 us

profile of v3, /device:TPU:0, one launch (start us, length us, event | category | flops | bytes accessed | tf_op | source)
XLA Modules:
  0.0 19.8 jit_solution(16918312838086522978)
XLA Ops:
  0.6 18.4 %shard_map.131 = (bf16[128,1024]{1,0:T(8,128)(2,1)S(1)}, bf16[32,1024]{1,0:T(8,128)(2,1)S(1)}) custom-call(bf16[128,1024]{1,0:T(8,128)(2,1)} %tokens_h.1, s32[1,4,16]{2,1,0:T(4,128)} %picks_h.1, f32[1,4,16]{2,1,0:T(4,128)} %gates_h.1, s32[1,4]{1,0:T(1,128)} %counts_h.1, f32[1,1024]{1,0:T(1,128)} %bitcast.2, f32[1,1024]{1,0:T(1,128)} %bitcast.3, ...), custom_call_target="tpu_custom_call" | custom-call | tf_op jit(solution)/shard_map/pallas_call | solution.py:435
  19.0 0.7 %shard_map.132 = (bf16[128,1024]{1,0:T(8,128)(2,1)}, bf16[32,1024]{1,0:T(8,128)(2,1)}) custom-call(bf16[128,1024]{1,0:T(8,128)(2,1)S(1)} %get-tuple-element.4.enc_v, bf16[32,1024]{1,0:T(8,128)(2,1)S(1)} %get-tuple-element.5.dec_v), custom_call_target="tpu_custom_call" | custom-call | tf_op jit(solution)/shard_map/pallas_call | solution.py:492

commit v4 on v3

--- a/solution.py
+++ b/solution.py
@@ -234,16 +234,11 @@
     position_three = lax.broadcasted_iota(jnp.int32, (rows, 3 * n_e * slots), 0)
     combine = jnp.where(position_three == pick_three, gate_three, 0.0).astype(BF16)
 
-    def feed(first, many, second=0, more=0):
+    def feed(first, many):
         flat = recv_a[first : first + many].reshape(many * slots, width)
-        if more:
-            rest = recv_a[second : second + more].reshape(more * slots, width)
-            flat = jnp.concatenate([flat, rest], axis=0)
         hidden = gelu(jnp.dot(flat, w_in_v[...], preferred_element_type=F32)).astype(BF16)
         result = jnp.dot(hidden, w_out_v[...], preferred_element_type=F32).astype(BF16)
-        send_b[first : first + many] = result[: many * slots].reshape(many, slots, width)
-        if more:
-            send_b[second : second + more] = result[many * slots :].reshape(more, slots, width)
+        send_b[first : first + many] = result.reshape(many, slots, width)
 
     loads["w_in"].wait()
     loads["w_out"].wait()
@@ -252,20 +247,13 @@
     near = [whole(recv_a, slot, 1, a_recv.at[slot]) for slot in range(own)]
     far_own = whole(recv_a, far, 1, a_recv.at[far])
     far_aside = whole(recv_a, extra, 1, a_recv.at[extra])
-    together = helper * lax.div(2 * me_e, n_e) * (1 - lax.div(me_e + 1, n_e))
-
-    @pl.when(together == 1)
-    def _():
-        for copy in near:
+    upper = lax.div(2 * me_e, n_e)
+
+    def feed_far():
+        for slot, copy in ((far, far_own), (extra, far_aside)):
             copy.wait()
-        far_own.wait()
-        feed(0, own, far, 1)
-        copy_b(far).start()
-        for slot in range(own):
+            feed(slot, 1)
             copy_b(slot).start()
-        far_aside.wait()
-        feed(extra, 1)
-        copy_b(extra).start()
 
     @pl.when(helper == 0)
     def _():
@@ -274,7 +262,11 @@
             feed(slot, 1)
             copy_b(slot).start()
 
-    @pl.when(helper - together == 1)
+    @pl.when(helper * upper == 1)
+    def _():
+        feed_far()
+
+    @pl.when(helper == 1)
     def _():
         for copy in near:
             copy.wait()
@@ -282,15 +274,9 @@
         for slot in range(own):
             copy_b(slot).start()
 
-
-    @pl.when(helper - together == 1)
+    @pl.when(helper * (1 - upper) == 1)
     def _():
-        far_own.wait()
-        feed(far, 1)
-        copy_b(far).start()
-        far_aside.wait()
-        feed(extra, 1)
-        copy_b(extra).start()
+        feed_far()
 
     both["w_kv"].wait()
     whole(q_v, 0, n_s - 1, q_recv.at[0]).wait()

time: 19.9 us -> 19.7 us (0.990)
  Pallas kernels: 19.1 us -> 18.9 us
where the time goes in v4:
time: 19.7 us; the launch traced here: 19.6 us
  Pallas kernels  18.9 us (96%)
  between operations  0.64 us (3%)
    pallas_call x1, Pallas kernels, local(): pl.pallas_call(functools.partial(kernel, n_e, n_s), out_shape=(pltpu.VMEM...  18.2 us
    pallas_call x1, Pallas kernels, local(): pl.pallas_call(finish, out_shape=(jax.ShapeDtypeStruct((rows, width), BF1...  0.74 us

profile of v4, /device:TPU:0, one launch (start us, length us, event | category | flops | bytes accessed | tf_op | source)
XLA Modules:
  0.0 19.6 jit_solution(9023444351850204915)
XLA Ops:
  0.6 18.2 %shard_map.131 = (bf16[128,1024]{1,0:T(8,128)(2,1)S(1)}, bf16[32,1024]{1,0:T(8,128)(2,1)S(1)}) custom-call(bf16[128,1024]{1,0:T(8,128)(2,1)} %tokens_h.1, s32[1,4,16]{2,1,0:T(4,128)} %picks_h.1, f32[1,4,16]{2,1,0:T(4,128)} %gates_h.1, s32[1,4]{1,0:T(1,128)} %counts_h.1, f32[1,1024]{1,0:T(1,128)} %bitcast.2, f32[1,1024]{1,0:T(1,128)} %bitcast.3, ...), custom_call_target="tpu_custom_call" | custom-call | tf_op jit(solution)/shard_map/pallas_call | solution.py:421
  18.8 0.7 %shard_map.132 = (bf16[128,1024]{1,0:T(8,128)(2,1)}, bf16[32,1024]{1,0:T(8,128)(2,1)}) custom-call(bf16[128,1024]{1,0:T(8,128)(2,1)S(1)} %get-tuple-element.4.enc_v, bf16[32,1024]{1,0:T(8,128)(2,1)S(1)} %get-tuple-element.5.dec_v), custom_call_target="tpu_custom_call" | custom-call | tf_op jit(solution)/shard_map/pallas_call | solution.py:478

commit v5 on v4

--- a/solution.py
+++ b/solution.py
@@ -1,4 +1,5 @@
 import functools
+import math
 
 import jax
 import jax.numpy as jnp
@@ -76,9 +77,7 @@
     load_sem,
     a_send,
     a_recv,
-    b_send,
     b_recv,
-    q_send,
     q_recv,
     p_send,
     p_recv,
@@ -173,7 +172,7 @@
         return remote(
             send_b.at[slot],
             recv_b.at[me_e],
-            b_send.at[1 if slot >= far else 0],
+            a_send.at[0],
             b_recv.at[0],
             peer(n_e, me_e, 0 if slot >= far else slot + 1),
             me_s - aside,
@@ -185,7 +184,7 @@
 
     def copy_q(d):
         to = lax.rem(me_s + d, n_s)
-        return remote(q_v.at[me_s], q_v.at[me_s], q_send.at[0], q_recv.at[0], me_e, to)
+        return remote(q_v.at[me_s], q_v.at[me_s], a_send.at[0], q_recv.at[0], me_e, to)
 
     def copy_p(d):
         to = lax.rem(me_s + d, n_s)
@@ -268,10 +267,9 @@
 
     @pl.when(helper == 1)
     def _():
-        for copy in near:
-            copy.wait()
-        feed(0, own)
-        for slot in range(own):
+        for slot in reversed(range(own)):
+            near[slot].wait()
+            feed(slot, 1)
             copy_b(slot).start()
 
     @pl.when(helper * (1 - upper) == 1)
@@ -300,6 +298,7 @@
     only = [jnp.where(lane_head == h, 1.0, 0.0).astype(BF16) for h in range(group)]
     slabs = [slice(g * slab, (g + 1) * slab) for g in range(groups)]
     keys = jnp.dot(encoded, w_kv_v[0], preferred_element_type=F32).astype(BF16)
+    values = jnp.dot(encoded, w_kv_v[1], preferred_element_type=F32).astype(BF16)
     scores = []
     for cols in slabs:
         key_heads = jnp.concatenate([keys[:, cols] * m for m in only], axis=0)
@@ -307,16 +306,15 @@
             lax.dot_general(
                 queries[:, cols], key_heads, (((1,), (1,)), ((), ())), preferred_element_type=F32
             )
-            * (head**-0.5)
-        )
-    values = jnp.dot(encoded, w_kv_v[1], preferred_element_type=F32).astype(BF16)
+        )
+    sharpness = head**-0.5 * math.log2(math.e)
     tops, totals = [], []
     for cols, score in zip(slabs, scores):
         weights = []
         for h in range(group):
             span = score[:, h * rows : (h + 1) * rows]
             row_max = jnp.max(span, axis=1, keepdims=True)
-            weight = jnp.exp(span - row_max)
+            weight = jnp.exp2((span - row_max) * sharpness)
             tops.append(row_max)
             totals.append(jnp.sum(weight, axis=1, keepdims=True))
             weights.append(weight.astype(BF16))
@@ -336,20 +334,28 @@
                 piece = jnp.where(stat_lane == lane + HEADS, totals[h][at : at + 8], piece)
             packed = packed + piece
         stat_v[s] = packed
-    for d in range(1, n_s):
-        copy_t(d).start()
-        copy_p(d).start()
+    for k in range(1, n_s // 2):
+        for core in range(2):
+            to = 2 * lax.rem(lax.div(me_s, 2) + k, n_s // 2) + core
+            d = lax.rem(to - me_s + n_s, n_s)
+            copy_t(d).start()
+            copy_p(d).start()
+    d = lax.rem(n_s + 1 - 2 * helper, n_s)
+    copy_t(d).start()
+    copy_p(d).start()
     part_r[0] = part_v[me_s]
     stat_r[0] = stat_v[me_s]
 
-    whole(send_a, 0, n_e - 1, a_send.at[0]).wait()
-    whole(send_b, 0, own, b_send.at[0]).wait()
+    sent = ((n_e - 1 + own) * slots * width + (n_s - 1) * dec_rows * q_width) // width
+
+    @pl.when(helper == 0)
+    def _():
+        whole(w_out_v, 0, sent, a_send.at[0]).wait()
 
     @pl.when(helper == 1)
     def _():
-        whole(send_b, far, 2, b_send.at[1]).wait()
-
-    whole(q_v, 0, n_s - 1, q_send.at[0]).wait()
+        whole(w_out_v, 0, sent + 2 * slots, a_send.at[0]).wait()
+
     loads["w_proj"].wait()
     whole(stat_r, 1, n_s - 1, t_recv.at[0]).wait()
     stat = []
@@ -365,7 +371,7 @@
             )
         )
     top = functools.reduce(jnp.maximum, stat)
-    factor = [jnp.exp(s - top)[:, :HEADS] for s in stat]
+    factor = [jnp.exp2((s - top) * sharpness)[:, :HEADS] for s in stat]
     total = sum(f * s[:, HEADS : 2 * HEADS] for f, s in zip(factor, stat))
     for d in range(n_s):
         scale = factor[d] / total
@@ -449,8 +455,6 @@
             dma((10,)),
             dma((1,)),
             dma((n_e + 1,)),
-            dma((2,)),
-            dma((1,)),
             dma((1,)),
             dma((1,)),
             dma((1,)),

time: 19.7 us -> 19.5 us (0.990)
  Pallas kernels: 18.9 us -> 18.7 us
    pallas_call x1, Pallas kernels: 18.2 us -> 18 us  [local(): pl.pallas_call(functools.partial(kernel, n_e, n_s), out_shape=(pltpu.VMEM...]
where the time goes in v5:
time: 19.5 us; the launch traced here: 19.4 us
  Pallas kernels  18.7 us (96%)
  between operations  0.64 us (3%)
    pallas_call x1, Pallas kernels, local(): pl.pallas_call(functools.partial(kernel, n_e, n_s), out_shape=(pltpu.VMEM...  18 us
    pallas_call x1, Pallas kernels, local(): pl.pallas_call(finish, out_shape=(jax.ShapeDtypeStruct((rows, width), BF1...  0.74 us

profile of v5, /device:TPU:0, one launch (start us, length us, event | category | flops | bytes accessed | tf_op | source)
XLA Modules:
  0.0 19.4 jit_solution(16355313934834081027)
XLA Ops:
  0.6 18.0 %shard_map.131 = (bf16[128,1024]{1,0:T(8,128)(2,1)S(1)}, bf16[32,1024]{1,0:T(8,128)(2,1)S(1)}) custom-call(bf16[128,1024]{1,0:T(8,128)(2,1)} %tokens_h.1, s32[1,4,16]{2,1,0:T(4,128)} %picks_h.1, f32[1,4,16]{2,1,0:T(4,128)} %gates_h.1, s32[1,4]{1,0:T(1,128)} %counts_h.1, f32[1,1024]{1,0:T(1,128)} %bitcast.2, f32[1,1024]{1,0:T(1,128)} %bitcast.3, ...), custom_call_target="tpu_custom_call" | custom-call | tf_op jit(solution)/shard_map/pallas_call | solution.py:427
  18.6 0.7 %shard_map.132 = (bf16[128,1024]{1,0:T(8,128)(2,1)}, bf16[32,1024]{1,0:T(8,128)(2,1)}) custom-call(bf16[128,1024]{1,0:T(8,128)(2,1)S(1)} %get-tuple-element.4.enc_v, bf16[32,1024]{1,0:T(8,128)(2,1)S(1)} %get-tuple-element.5.dec_v), custom_call_target="tpu_custom_call" | custom-call | tf_op jit(solution)/shard_map/pallas_call | solution.py:482
